TPU v7x, 32 devices: a whole 2x2x4 slice. The times are simulated.
32 devices in a mesh: groups: 2 (over y), space: 4 (over z), mp: 2 (over x), sub: 2 (over core).
Axes of the slice: x: 2, y: 2, z: 4, core: 2. Of those that a mesh axis runs over, the one named last changes fastest.
Arguments:
- voxels: bfloat16 [24576, 512], P(('groups', 'space', 'sub')), parts along dimension 0, may hold values from -6 to 6
- window_ids: int32 [24576], P(('groups', 'space', 'sub')), parts along dimension 0, may hold values from 0 to 127, as said below
- voxel_slots: int32 [24576], P(('groups', 'space', 'sub')), parts along dimension 0, may hold values from 0 to 255, as said below
- window_counts: int32 [256], P('groups'), parts along dimension 0, may hold values from 0 to 256, as said below
- norm_gain: float32 [512], replicated, may hold values from 0.25 to 1.75
- w_query_key: bfloat16 [2, 512, 512], P(None, None, 'mp'), may hold values from -2 to 2
- w_value: bfloat16 [512, 512], P(None, 'mp'), may hold values from -0.25 to 0.25
- w_out: bfloat16 [512, 512], P('mp'), may hold values from -0.25 to 0.25
- ffn_gain: float32 [512], replicated, may hold values from 0.25 to 1.75
- w_up: bfloat16 [512, 2048], P(None, 'mp'), may hold values from -0.25 to 0.25
- w_down: bfloat16 [2048, 512], P('mp'), may hold values from -0.125 to 0.125
Outputs:
- result: bfloat16 [24576, 512], P(('groups', 'space', 'sub'), 'mp'), parts along dimension 0
There are 2 independent parts, one for each index of `groups`. A program takes and returns all parts, laid end to end along the dimension named above; an argument that names none is the same for every part. Nothing has to cross between parts.
Inputs may be any that keep to these rules, and one draw needn't show every extreme that they name: `window_ids`: window w belongs to owner w // 16 (its index along space+sub) as that owner's window w % 16. On the voxels of one device at most 384 lie in windows of one owner, and in every draw some owner has exactly 384 voxels of every device. `voxel_slots`: the voxels of a window hold slots 0 to its count - 1, each once. window_counts[w] is the number of voxels with window id w; some window holds 256.
All inputs are finite; a program needn't handle non-finite values.
Results may differ from a plain program's by a relative error of at most 0.012.
Values may be sent and summed in bfloat16 or wider, within the bound.
A program may use at most 128 MiB of HBM per device.

v0:
```python
import jax
import jax.numpy as jnp
from jax import lax
from jax.sharding import PartitionSpec as P

HDIM = 64
WLEN = 256
WIN_DEV = 16


def normalize(values_in, gain):
    row_mean = jnp.mean(values_in, axis=-1, keepdims=True)
    centred = values_in - row_mean
    variance = jnp.mean(centred * centred, axis=-1, keepdims=True)
    return centred * lax.rsqrt(variance + 1e-05) * gain


def project(rows_in, weight):
    return jnp.dot(rows_in, weight, preferred_element_type=jnp.float32).astype(jnp.bfloat16)


def feed_forward(normed_in, up_proj, down_proj):
    hidden = jax.nn.gelu(
        jnp.dot(normed_in, up_proj, preferred_element_type=jnp.float32), approximate=True
    ).astype(jnp.bfloat16)
    return jnp.dot(hidden, down_proj, preferred_element_type=jnp.float32)


def regroup(send_rows, send_spots):
    return (
        lax.all_to_all(send_rows, ("space", "sub"), split_axis=0, concat_axis=0, tiled=True),
        lax.all_to_all(send_spots, ("space", "sub"), split_axis=0, concat_axis=0, tiled=True),
    )


def send_back(send_rows):
    return lax.all_to_all(send_rows, ("space", "sub"), split_axis=0, concat_axis=0, tiled=True)


def attend(queries, key_rows, values, counts):
    windows = counts.shape[0]
    window_len = queries.shape[0] // windows
    head_count = queries.shape[1] // HDIM
    split_shape = (windows, window_len, head_count, HDIM)
    scores = jnp.einsum(
        "wqhd,wkhd->whqk",
        queries.reshape(split_shape),
        key_rows.reshape(split_shape),
        preferred_element_type=jnp.float32,
    ) * HDIM ** (-0.5)
    live_keys = (jnp.arange(window_len, dtype=jnp.int32)[None, :] < counts[:, None])[
        :, None, None, :
    ]
    scores = jnp.where(live_keys, scores, jnp.float32(-1e30))
    row_max = jnp.max(scores, axis=-1, keepdims=True)
    weights = jnp.exp(scores - row_max)
    probabilities = (weights / jnp.sum(weights, axis=-1, keepdims=True)).astype(jnp.bfloat16)
    mixture = jnp.einsum(
        "whqk,wkhd->wqhd",
        probabilities,
        values.reshape(split_shape),
        preferred_element_type=jnp.float32,
    )
    return mixture.astype(jnp.bfloat16).reshape(windows * window_len, head_count * HDIM)


def shards(
    voxels,
    window_ids,
    voxel_slots,
    window_counts,
    norm_gain,
    w_query_key,
    w_value,
    w_out,
    ffn_gain,
    w_up,
    w_down,
):
    owner_total = lax.axis_size(("space", "sub"))
    my_index = lax.axis_index(("space", "sub"))
    row_count = voxels.shape[0]
    capacity = 2 * row_count // owner_total
    local_width = w_value.shape[1]
    stream = voxels.astype(jnp.float32)
    normed = normalize(stream, norm_gain).astype(jnp.bfloat16)
    destination = window_ids // WIN_DEV
    position = window_ids % WIN_DEV * WLEN + voxel_slots
    target = (destination[:, None] == jnp.arange(owner_total, dtype=jnp.int32)[None, :]).astype(
        jnp.int32
    )
    before = jnp.sum((jnp.cumsum(target, axis=0) - target) * target, axis=1)
    send_index = destination * capacity + before
    row_width = normed.shape[1]
    outgoing = (
        jnp.zeros((owner_total * capacity, row_width), jnp.bfloat16).at[send_index].set(normed)
    )
    out_spots = (
        jnp.full((owner_total * capacity,), WIN_DEV * WLEN, jnp.int32).at[send_index].set(position)
    )
    arrived, arrived_spots = regroup(
        outgoing.reshape(owner_total, capacity, row_width), out_spots.reshape(owner_total, capacity)
    )
    arrived = arrived.reshape(owner_total * capacity, row_width)
    arrived_spots = arrived_spots.reshape(owner_total * capacity)
    padded = (
        jnp.zeros((WIN_DEV * WLEN, row_width), jnp.bfloat16)
        .at[arrived_spots]
        .set(arrived, mode="drop")
    )
    queries = project(padded, w_query_key[0])
    key_rows = project(padded, w_query_key[1])
    values = project(padded, w_value)
    counts = lax.dynamic_slice_in_dim(window_counts, my_index * WIN_DEV, WIN_DEV, 0)
    mixture = attend(queries, key_rows, values, counts)
    answer = jnp.take(mixture, arrived_spots, axis=0, mode="clip").reshape(
        owner_total, capacity, local_width
    )
    answer = send_back(answer)
    attended = answer.reshape(owner_total * capacity, local_width)[send_index]
    head_rows = w_out.shape[0]
    all_heads, whole_out = (
        lax.all_gather(attended, "mp", axis=1, tiled=True),
        lax.all_gather(w_out, "mp", axis=0, tiled=True),
    )
    after_attn = stream + jnp.dot(all_heads, whole_out, preferred_element_type=jnp.float32)
    ffn_terms = feed_forward(normalize(after_attn, ffn_gain).astype(jnp.bfloat16), w_up, w_down)
    remainder = lax.dynamic_slice_in_dim(after_attn, lax.axis_index("mp") * head_rows, head_rows, 1)
    result = (
        lax.psum_scatter(
            ffn_terms.astype(jnp.bfloat16), "mp", scatter_dimension=1, tiled=True
        ).astype(jnp.float32)
        + remainder
    )
    return result.astype(jnp.bfloat16)


def solution(mesh):
    return jax.shard_map(
        shards,
        mesh=mesh,
        in_specs=(
            P(("groups", "space", "sub"), None),
            P(("groups", "space", "sub")),
            P(("groups", "space", "sub")),
            P("groups"),
            P(),
            P(None, None, "mp"),
            P(None, "mp"),
            P("mp", None),
            P(),
            P(None, "mp"),
            P("mp", None),
        ),
        out_specs=P(("groups", "space", "sub"), "mp"),
        check_vma=False,
    )
```

profile of v0, /device:TPU:30, one launch (start us, length us, event | category | flops | bytes accessed | tf_op | source)
XLA Modules:
  0.0 338.5 jit_solution(189395623815067375)
XLA Ops:
  7.4 2.3 reduce-window.6
  10.3 6.8 %scatter_custom_fusion = s32[3072]{0:T(1024)} fusion(s32[1536]{0:T(1024)S(1)} %compare_select_fusion.1, s32[1536]{0:T(1024)S(1)} %get-tuple-element.5, s32[]{:T(128)} %constant.31.clone.1), kind=kCustom, calls=%fused_computation.79 | custom fusion | bytes 12292 | tf_op jit(solution)/shard_map/scatter | solution.py:99
  17.0 5.1 %all-to-all-start = ((s32[8,1,384]{2,1,0:T(1,128)}), s32[8,1,384]{2,1,0:T(1,128)S(1)}, u32[]{:S(2)}, u32[]{:S(2)}) async-start(s32[8,1,384]{2,1,0:T(1,128)} %bitcast.2), calls=%async_computation | async-start | bytes 24576 | tf_op jit(solution)/shard_map/all_to_all | solution.py:32
  22.1 1.7 copy.19
  24.6 1.6 fusion.22
  26.2 2.6 copy.20
  28.8 9.9 %scatter_custom_fusion.1 = bf16[3072,512]{1,0:T(8,128)(2,1)} fusion(s32[1536]{0:T(1024)S(1)} %compare_select_fusion.1, bf16[1536,512]{1,0:T(8,128)(2,1)} %copy.20, bf16[]{:T(256)} %constant.28.clone.1), kind=kCustom, calls=%fused_computation.48 | custom fusion | bytes 3146240 | tf_op jit(solution)/shard_map/scatter | solution.py:96
  38.7 5.2 %all-to-all-start.1 = ((bf16[8,384,512]{2,1,0:T(8,128)(2,1)}), bf16[8,384,512]{2,1,0:T(8,128)(2,1)}, u32[]{:S(2)}, u32[]{:S(2)}) async-start(bf16[8,384,512]{2,1,0:T(8,128)(2,1)} %bitcast.45), calls=%async_computation.1 | async-start | bytes 6291456 | tf_op jit(solution)/shard_map/all_to_all | solution.py:31
  44.1 68.9 %all-to-all-done.1 = bf16[8,384,512]{2,1,0:T(8,128)(2,1)} async-done(((bf16[8,384,512]{2,1,0:T(8,128)(2,1)}), bf16[8,384,512]{2,1,0:T(8,128)(2,1)}, u32[]{:S(2)}, u32[]{:S(2)}) %all-to-all-start.1) | async-done | bytes 3145760 | tf_op jit(solution)/shard_map/all_to_all | solution.py:31
  113.0 16.9 %scatter_custom_fusion.2 = bf16[4096,512]{1,0:T(8,128)(2,1)} fusion(s32[3072]{0:T(1024)S(1)} %bitcast.51, bf16[3072,512]{1,0:T(8,128)(2,1)} %bitcast.6, bf16[]{:T(256)} %constant.28.clone.1), kind=kCustom, calls=%fused_computation.42 | custom fusion | bytes 4194816 | tf_op jit(solution)/shard_map/scatter | solution.py:109
  129.9 4.9 %convolution_convert_fusion.1 = bf16[4096,256]{1,0:T(8,128)(2,1)} fusion(bf16[4096,512]{1,0:T(8,128)(2,1)} %scatter_custom_fusion.2, bf16[2,512,256]{2,1,0:T(8,128)(2,1)S(1)} %copy-done.7), kind=kOutput, calls=%fused_computation.24 | convolution fusion | flops 1074790400 | bytes 6553600 | tf_op jit(solution)/shard_map/dot_general | solution.py:19
  134.8 1.3 convolution_convert_fusion
  136.1 7.1 %reshape.179 = bf16[16,256,4,64]{3,2,1,0:T(4,128)(2,1)} reshape(bf16[4096,256]{1,0:T(8,128)(2,1)} %convolution_convert_fusion.1) | data formatting | bytes 4194304 | tf_op jit(solution)/shard_map/reshape | solution.py:47
  143.2 3.2 reshape.180
  146.4 3.4 %convolution_convert_fusion.2 = bf16[4096,256]{1,0:T(8,128)(2,1)S(1)} fusion(bf16[4096,512]{1,0:T(8,128)(2,1)} %scatter_custom_fusion.2, bf16[512,256]{1,0:T(8,128)(2,1)S(1)} %copy-done.9), kind=kOutput, calls=%fused_computation.25 | convolution fusion | flops 1074790400 | bytes 6553600 | tf_op jit(solution)/shard_map/dot_general | solution.py:19
  149.9 3.3 reshape.178
  153.1 11.5 %fusion.14 = f32[16,4,256,256]{2,3,1,0:T(8,128)} fusion(bf16[16,256,4,64]{3,2,1,0:T(4,128)(2,1)} %reshape.180, bf16[16,256,4,64]{3,2,1,0:T(4,128)(2,1)} %reshape.179), kind=kOutput, calls=%fused_computation.29 | convolution fusion | flops 536870912 | bytes 20971520 | tf_op jit(solution)/shard_map/wqhd,wkhd->whqk/dot_general | solution.py:45
  164.7 18.8 %fusion.52 = (f32[16,4,256]{2,1,0:T(4,128)S(1)}, f32[16,4,256,256]{2,3,1,0:T(8,128)}) fusion(f32[16,4,256,256]{2,3,1,0:T(8,128)} %fusion.14, pred[16,256]{1,0:T(8,128)(4,1)S(1)} %iota_compare_fusion.2), kind=kOutput, calls=%fused_computation.90 | output fusion | flops 25166080 | bytes 33624064 | tf_op jit(solution)/shard_map/sub | solution.py:56
  183.5 9.0 %convert_bitcast_fusion = bf16[16,256,4,64]{1,3,2,0:T(8,128)(2,1)S(1)} fusion(f32[16,4,256,256]{2,3,1,0:T(8,128)} %get-tuple-element.8, f32[16,4,256]{2,1,0:T(4,128)S(1)} %get-tuple-element.7, bf16[16,256,4,64]{3,2,1,0:T(4,128)(2,1)} %reshape.178), kind=kOutput, calls=%fused_computation.41 | convolution fusion | flops 546308096 | bytes 21037056 | tf_op jit(solution)/shard_map/whqk,wkhd->wqhd/dot_general | solution.py:58
  192.4 4.6 %copy.40 = bf16[16,256,4,64]{3,2,1,0:T(4,128)(2,1)} copy(bf16[16,256,4,64]{1,3,2,0:T(8,128)(2,1)S(1)} %convert_bitcast_fusion) | data formatting | bytes 4194304 | tf_op jit(solution)/shard_map/reshape | solution.py:64
  197.1 6.0 %reshape.181 = bf16[4096,256]{1,0:T(8,128)(2,1)S(1)} reshape(bf16[16,256,4,64]{3,2,1,0:T(4,128)(2,1)} %copy.40) | data formatting | bytes 4194304 | tf_op jit(solution)/shard_map/reshape | solution.py:64
  203.0 13.0 %gather_fusion = bf16[3072,256]{1,0:T(8,128)(2,1)} fusion(bf16[4096,256]{1,0:T(8,128)(2,1)S(1)} %reshape.181, s32[3072]{0:T(1024)S(1)} %broadcast_clamp_fusion), kind=kCustom, calls=%fused_computation | custom fusion | bytes 3158016 | tf_op jit(solution)/shard_map/jit(_take)/gather | solution.py:116
  216.0 6.1 %all-to-all-start.2 = ((bf16[8,384,256]{2,1,0:T(8,128)(2,1)}), bf16[8,384,256]{2,1,0:T(8,128)(2,1)S(1)}, u32[]{:S(2)}, u32[]{:S(2)}) async-start(bf16[8,384,256]{2,1,0:T(8,128)(2,1)} %bitcast.46), calls=%async_computation.2 | async-start | bytes 3145728 | tf_op jit(solution)/shard_map/all_to_all | solution.py:37
  222.1 35.2 %all-to-all-done.2 = bf16[8,384,256]{2,1,0:T(8,128)(2,1)S(1)} async-done(((bf16[8,384,256]{2,1,0:T(8,128)(2,1)}), bf16[8,384,256]{2,1,0:T(8,128)(2,1)S(1)}, u32[]{:S(2)}, u32[]{:S(2)}) %all-to-all-start.2) | async-done | bytes 1572896 | tf_op jit(solution)/shard_map/all_to_all | solution.py:37
  257.3 5.4 %gather_fusion.1 = bf16[1536,256]{1,0:T(8,128)(2,1)} fusion(bf16[3072,256]{1,0:T(8,128)(2,1)S(1)} %bitcast.44, s32[2048]{0:T(1024)S(1)} %pad_clamp_fusion), kind=kCustom, calls=%fused_computation.1 | custom fusion | bytes 1579008 | tf_op jit(solution)/shard_map/gather | solution.py:120
  262.7 8.9 %all_gather.7 = bf16[512,512]{1,0:T(8,128)(2,1)S(1)} all-gather(bf16[256,512]{1,0:T(8,128)(2,1)S(1)} %copy-done.4), channel_id=1, replica_groups=mesh['groups'=2,'space'=4,'mp'=2,'sub'=2] {'mp'}, dimensions={0}, use_global_device_ids=true | all-gather | bytes 786432 | tf_op jit(solution)/shard_map/all_gather | solution.py:124
  271.7 18.3 %all-gather.3.cloned.1.call-done = bf16[1536,512]{1,0:T(8,128)(2,1)} async-done(((bf16[1536,256]{1,0:T(8,128)(2,1)}), bf16[1536,512]{1,0:T(8,128)(2,1)}) %all-gather.3.cloned.1.call-update) | async-done | bytes 1572880 | tf_op jit(solution)/shard_map/all_gather | solution.py:123
  290.0 2.9 fusion.53
  293.0 1.6 copy-done.2
  295.0 7.4 %convolution_convert_fusion.3 = bf16[1536,512]{0,1:T(8,128)(2,1)} fusion(bf16[1024,512]{1,0:T(8,128)(2,1)S(1)} %copy-done, bf16[512,1024]{1,0:T(8,128)(2,1)S(1)} %copy-done.6, f32[1536,512]{0,1:T(8,128)} %copy-done.2, f32[512]{0:T(512)S(1)} %copy-done.10, f32[1536]{0:T(1024)S(1)} %add_rsqrt_fusion, f32[1536]{0:T(1024)S(1)} %broadcast_multiply_fusion), kind=kOutput, calls=%fused_computation.40 | convolution fusion | flops 3239313408 | bytes 6830080 | tf_op jit(solution)/shard_map/dot_general | solution.py:26
  302.4 26.3 %reduce-scatter.2.cloned.1.call-done = bf16[1536,256]{0,1:T(8,128)(2,1)} async-done(((bf16[1536,512]{0,1:T(8,128)(2,1)}), bf16[1536,256]{0,1:T(8,128)(2,1)}) %reduce-scatter.2.cloned.1.call-update) | async-done | bytes 786448 | tf_op jit(solution)/shard_map/reduce_scatter | solution.py:130
  328.7 1.8 add_convert_fusion
  (48 shorter events, 4.0 us)
Async XLA Ops:
  6.5 288.5 %copy-start = (bf16[1024,512]{1,0:T(8,128)(2,1)S(1)}, bf16[1024,512]{1,0:T(8,128)(2,1)}, u32[]{:S(2)}) copy-start(bf16[1024,512]{1,0:T(8,128)(2,1)} %param.21) | copy-start | bytes 3145732
  17.0 21.7 %all-to-all-start = ((s32[8,1,384]{2,1,0:T(1,128)}), s32[8,1,384]{2,1,0:T(1,128)S(1)}, u32[]{:S(2)}, u32[]{:S(2)}) async-start(s32[8,1,384]{2,1,0:T(1,128)} %bitcast.2), calls=%async_computation | async-start | bytes 24576 | tf_op jit(solution)/shard_map/all_to_all | solution.py:32
  22.1 2.5 copy-start.5
  23.8 2.4 copy-start.1
  38.7 5.2 %copy-start.11 = (s32[128]{0:T(128)S(1)}, s32[128]{0:T(128)}, u32[]{:S(2)}) copy-start(s32[128]{0:T(128)} %param.14) | copy-start | bytes 1540
  38.7 74.3 %all-to-all-start.1 = ((bf16[8,384,512]{2,1,0:T(8,128)(2,1)}), bf16[8,384,512]{2,1,0:T(8,128)(2,1)}, u32[]{:S(2)}, u32[]{:S(2)}) async-start(bf16[8,384,512]{2,1,0:T(8,128)(2,1)} %bitcast.45), calls=%async_computation.1 | async-start | bytes 6291456 | tf_op jit(solution)/shard_map/all_to_all | solution.py:31
  43.9 86.0 %copy-start.7 = (bf16[2,512,256]{2,1,0:T(8,128)(2,1)S(1)}, bf16[2,512,256]{2,1,0:T(8,128)(2,1)}, u32[]{:S(2)}) copy-start(bf16[2,512,256]{2,1,0:T(8,128)(2,1)} %param.16) | copy-start | bytes 1572868
  129.9 4.9 %copy-start.3 = (bf16[4096,512]{1,0:T(8,128)(2,1)S(1)}, bf16[4096,512]{1,0:T(8,128)(2,1)}, u32[]{:S(2)}) copy-start(bf16[4096,512]{1,0:T(8,128)(2,1)} %scatter_custom_fusion.2) | copy-start | bytes 12582916
  129.9 4.9 %copy-start.8 = (bf16[2,512,256]{2,1,0:T(8,128)(2,1)S(1)}, bf16[2,512,256]{2,1,0:T(8,128)(2,1)}, u32[]{:S(2)}) copy-start(bf16[2,512,256]{2,1,0:T(8,128)(2,1)} %param.16) | copy-start | bytes 1572868
  143.2 3.2 copy-start.9
  216.0 41.3 %all-to-all-start.2 = ((bf16[8,384,256]{2,1,0:T(8,128)(2,1)}), bf16[8,384,256]{2,1,0:T(8,128)(2,1)S(1)}, u32[]{:S(2)}, u32[]{:S(2)}) async-start(bf16[8,384,256]{2,1,0:T(8,128)(2,1)} %bitcast.46), calls=%async_computation.2 | async-start | bytes 3145728 | tf_op jit(solution)/shard_map/all_to_all | solution.py:37
  222.0 67.9 %all-gather.3.cloned.1.call-start = ((), (), s32[]{:S(2)}) async-start(), calls=%async_computation.5 | async-start | bytes 2359296 | tf_op jit(solution)/shard_map/all_gather | solution.py:123
  257.3 5.4 %copy-start.4 = (bf16[256,512]{1,0:T(8,128)(2,1)S(1)}, bf16[256,512]{1,0:T(8,128)(2,1)}, u32[]{:S(2)}) copy-start(bf16[256,512]{1,0:T(8,128)(2,1)} %param.18) | copy-start | bytes 786436
  262.7 66.1 %reduce-scatter.2.cloned.1.call-start = ((), (), s32[]{:S(2)}) async-start(), calls=%async_computation.4 | async-start | bytes 2359296 | tf_op jit(solution)/shard_map/reduce_scatter | solution.py:130
  292.9 1.7 copy-start.2
  292.9 2.1 copy-start.6
  292.9 2.1 copy-start.10
Sparse Core Ops, SparseCore 0:
  262.8 27.1 all-gather.2
  302.6 26.1 reduce-scatter.1
where the time goes:
time: 342 us; the launch traced here: 339 us
  waiting for transfers between devices  149 us (44%)
  local copies, waits for them, and re-layouts  83.5 us (24%)
  matrix products  40.4 us (12%)
  other arithmetic  26.9 us (8%)
  starting transfers between devices  16.4 us (5%)
  between operations  13.6 us (4%)
  blocking collectives  8.94 us (3%)
    all_to_all x1, waiting for transfers between devices, regroup(): lax.all_to_all(send_rows, ('space', 'sub'), split_axis=0, concat_axis=0,...  68.9 us
    all_to_all x1, waiting for transfers between devices, send_back(): lax.all_to_all(send_rows, ('space', 'sub'), split_axis=0, concat_axis=0,...  35.2 us
    reduce_scatter x1, waiting for transfers between devices, shards(): lax.psum_scatter(ffn_terms.astype(jnp.bfloat16), 'mp', scatter_dimension=...  26.3 us
    sub x1, other arithmetic, attend(): weights = jnp.exp(scores - row_max)  18.8 us
    all_gather x1, waiting for transfers between devices, shards(): lax.all_gather(attended, 'mp', axis=1, tiled=True)  18.3 us
    scatter x1, local copies, waits for them, and re-layouts, shards(): padded = jnp.zeros((WIN_DEV * WLEN, row_width), jnp.bfloat16).at[arrived_...  16.9 us
    gather x1, local copies, waits for them, and re-layouts, shards(): jnp.take(mixture, arrived_spots, axis=0, mode='clip')  13 us
    dot_general x1, matrix products, attend(): jnp.einsum('wqhd,wkhd->whqk', queries.reshape(split_shape), key_rows.resh...  11.5 us
  transfers between devices with their start and end apart: 5, of which 4 were waited for; matrix products, arithmetic and copies ran while one was open for 5% of the time, Pallas kernels for 0%

commit v1 on v0

v1 whole, which is shorter than its diff:
```python
import functools
import math

import jax
import jax.numpy as jnp
from jax import lax
from jax.experimental import pallas as pl
from jax.experimental.pallas import tpu as pltpu
from jax.sharding import PartitionSpec as P

HDIM = 64
WLEN = 256
WIN_DEV = 16
BASE = 64
MESH = pl.DeviceIdType.MESH
VMEM = pl.BlockSpec(memory_space=pltpu.VMEM)
f32 = jnp.float32
bf16 = jnp.bfloat16


def normalize(values_in, gain):
    row_mean = jnp.mean(values_in, axis=-1, keepdims=True)
    centred = values_in - row_mean
    variance = jnp.mean(centred * centred, axis=-1, keepdims=True)
    return centred * lax.rsqrt(variance + 1e-05) * gain


def iota(shape, dim):
    return lax.broadcasted_iota(jnp.int32, shape, dim)


def one_hot(found):
    return jnp.where(found, f32(1), f32(0)).astype(bf16)


def dot(a, b, dims=((1,), (0,))):
    return lax.dot_general(a, b, (dims, ((), ())), preferred_element_type=f32)


def greet(owners, subs, mp_n, me, m):
    barrier = pltpu.get_barrier_semaphore()
    for k in range(1, owners):
        t = (me + k) % owners
        pl.semaphore_signal(
            barrier, inc=1, device_id={"space": t // subs, "sub": t % subs}, device_id_type=MESH
        )
    for p in range(1, mp_n):
        pl.semaphore_signal(
            barrier, inc=1, device_id={"mp": (m + p) % mp_n}, device_id_type=MESH
        )
    pl.semaphore_wait(barrier, owners - 1 + mp_n - 1)


def to_owner(src, dst, sems, slot, target, subs):
    return pltpu.make_async_remote_copy(
        src_ref=src,
        dst_ref=dst,
        send_sem=sems[0].at[slot],
        recv_sem=sems[1].at[slot],
        device_id={"space": target // subs, "sub": target % subs},
        device_id_type=MESH,
    )


def to_mp(src, dst, sems, index, peer):
    return pltpu.make_async_remote_copy(
        src_ref=src,
        dst_ref=dst,
        send_sem=sems[0].at[index],
        recv_sem=sems[1].at[index],
        device_id={"mp": peer},
        device_id_type=MESH,
    )


def relay(owners, subs, mp_n, me, m, outbuf, blocks, main, side):
    last = owners - 1

    def onward(slot, carry):
        s = (me + owners - slot - 1) % owners
        to_owner(outbuf.at[slot], blocks.at[m, s], main, slot, s, subs).wait_recv()
        for p in range(1, mp_n):
            to_mp(
                blocks.at[m, s], blocks.at[m, s], side, slot * (mp_n - 1) + p - 1, (m + p) % mp_n
            ).start()
        return carry

    for p in range(1, mp_n):
        to_mp(
            outbuf.at[last], blocks.at[m, me], side, last * (mp_n - 1) + p - 1, (m + p) % mp_n
        ).start()
    lax.fori_loop(0, last, onward, 0)

    def finish(slot, carry):
        s = (me + owners - slot - 1) % owners
        for p in range(1, mp_n):
            to_mp(
                outbuf.at[slot],
                blocks.at[(m + mp_n - p) % mp_n, s],
                side,
                slot * (mp_n - 1) + p - 1,
                (m + p) % mp_n,
            ).wait()
        return carry

    lax.fori_loop(0, owners, finish, 0)

    def sent(slot, carry):
        to_owner(outbuf.at[slot], blocks.at[m, me], main, slot, me, subs).wait_send()
        return carry

    lax.fori_loop(0, last, sent, 0)


def dispatch_kernel(
    owners, subs, mp_n, half, index, digits, out_rows, arrived, spots, whole_out,
    outbuf, spotbuf, ms, mr, ps, pr, ss, sr, ws, wr,
):
    me = lax.axis_index("space") * subs + lax.axis_index("sub")
    m = lax.axis_index("mp")
    cap, rows = outbuf.shape[1], half.shape[0]
    greet(owners, subs, mp_n, me, m)
    for p in range(1, mp_n):
        to_mp(out_rows, whole_out.at[m], (ws, wr), p - 1, (m + p) % mp_n).start()
    whole_out[m] = out_rows[...]

    def send(slot):
        t = (me + slot + 1) % owners
        to_owner(outbuf.at[slot], arrived.at[m, me], (ms, mr), slot, t, subs).start()
        to_owner(spotbuf.at[slot], spots.at[me], (ps, pr), slot, t, subs).start()

    def build(slot, carry):
        t = (me + slot + 1) % owners
        hit = one_hot(index[...] == iota((cap, rows), 0) + t * cap)
        outbuf[slot] = dot(hit, half[...]).astype(bf16)
        parts = dot(digits[...], hit, ((1,), (1,)))
        place = parts[0:1] * BASE + parts[1:2] + (1 - parts[2:3]) * (WIN_DEV * WLEN)
        spotbuf[slot] = place.astype(jnp.int32)

        @pl.when(slot > 0)
        def _():
            send(slot - 1)

        return carry

    lax.fori_loop(0, owners, build, 0)
    arrived[m, me] = outbuf[owners - 1]
    spots[me] = spotbuf[owners - 1]
    relay(owners, subs, mp_n, me, m, outbuf, arrived, (ms, mr), (ss, sr))

    def tail(slot, carry):
        s = (me + owners - slot - 1) % owners
        to_owner(spotbuf.at[slot], spots.at[s], (ps, pr), slot, s, subs).wait()
        return carry

    lax.fori_loop(0, owners - 1, tail, 0)
    for p in range(1, mp_n):
        to_mp(
            out_rows, whole_out.at[(m + mp_n - p) % mp_n], (ws, wr), p - 1, (m + p) % mp_n
        ).wait()


def dispatch(owners, subs, mp_n, cap, half, index, digits, out_rows):
    part = half.shape[1]
    dma = pltpu.SemaphoreType.DMA
    side = owners * (mp_n - 1)
    return pl.pallas_call(
        functools.partial(dispatch_kernel, owners, subs, mp_n),
        out_shape=(
            jax.ShapeDtypeStruct((mp_n, owners, cap, part), bf16),
            jax.ShapeDtypeStruct((owners, 1, cap), jnp.int32),
            jax.ShapeDtypeStruct((mp_n,) + out_rows.shape, bf16),
        ),
        in_specs=[VMEM] * 4,
        out_specs=(VMEM, VMEM, VMEM),
        scratch_shapes=[
            pltpu.VMEM((owners, cap, part), bf16),
            pltpu.VMEM((owners, 1, cap), jnp.int32),
            dma((owners,)), dma((owners,)), dma((owners,)), dma((owners,)),
            dma((side,)), dma((side,)), dma((mp_n,)), dma((mp_n,)),
        ],
        compiler_params=pltpu.CompilerParams(collective_id=0, has_side_effects=True),
        name="dispatch",
    )(half, index, digits, out_rows)


def attend_kernel(group, counts, spots, arrived, w_qk, w_v, mixture):
    step = pl.program_id(0)
    halves, total, part = arrived.shape
    local = w_v.shape[1]
    heads = local // HDIM
    slots = group * WLEN
    hit = one_hot(spots[...] == iota((slots, total), 0) + step * slots)
    rows_in = jnp.concatenate(
        [dot(hit, arrived[h]).astype(bf16) for h in range(halves)], axis=1
    )
    queries = dot(rows_in, w_qk[0]).astype(bf16)
    keys = dot(rows_in, w_qk[1]).astype(bf16)
    values = dot(rows_in, w_v[...]).astype(bf16)
    head_of = iota((1, local), 1) // HDIM
    masks = [jnp.where(head_of == h, f32(1), f32(0)).astype(bf16) for h in range(heads)]
    for g in range(group):
        span = slice(g * WLEN, (g + 1) * WLEN)
        q, k, v = queries[span], keys[span], values[span]
        stacked = jnp.concatenate([q * masks[h] for h in range(heads)], axis=0)
        scores = dot(stacked, k, ((1,), (1,))) * f32(HDIM ** -0.5)
        live = iota((1, WLEN), 1) < counts[step * group + g]
        scores = jnp.where(live, scores, f32(-1e30))
        weights = jnp.exp(scores - jnp.max(scores, axis=-1, keepdims=True))
        scale = 1.0 / jnp.sum(weights, axis=-1, keepdims=True)
        mixed = dot((weights * scale).astype(bf16), v)
        out = mixed[:WLEN]
        for h in range(1, heads):
            out = jnp.where(head_of == h, mixed[h * WLEN : (h + 1) * WLEN], out)
        mixture[span, :] = out.astype(bf16)


def attend(counts, spots, arrived, w_qk, w_v, group=2):
    local = w_v.shape[1]
    whole = lambda a: pl.BlockSpec(a.shape, lambda i: (0,) * a.ndim)
    return pl.pallas_call(
        functools.partial(attend_kernel, group),
        grid=(WIN_DEV // group,),
        out_shape=jax.ShapeDtypeStruct((WIN_DEV * WLEN, local), bf16),
        in_specs=[pl.BlockSpec(memory_space=pltpu.SMEM)]
        + [whole(a) for a in (spots, arrived, w_qk, w_v)],
        out_specs=pl.BlockSpec((group * WLEN, local), lambda i: (i, 0)),
        name="attend",
    )(counts, spots, arrived, w_qk, w_v)


def answer_kernel(owners, subs, mp_n, mixture, column, answers, outbuf, total, ms, mr, ss, sr):
    me = lax.axis_index("space") * subs + lax.axis_index("sub")
    m = lax.axis_index("mp")
    cap = outbuf.shape[1]
    span = 4 * WLEN
    greet(owners, subs, mp_n, me, m)

    def send(slot):
        t = (me + slot + 1) % owners
        to_owner(outbuf.at[slot], answers.at[m, me], (ms, mr), slot, t, subs).start()

    def build(slot, carry):
        t = (me + slot + 1) % owners
        place = column[t]
        total[...] = jnp.zeros_like(total)

        def add(c, inner):
            hit = one_hot(place == iota((cap, span), 1) + c * span)
            total[...] += dot(hit, mixture[pl.ds(c * span, span), :])
            return inner

        lax.fori_loop(0, mixture.shape[0] // span, add, 0)
        outbuf[slot] = total[...].astype(bf16)

        @pl.when(slot > 0)
        def _():
            send(slot - 1)

        return carry

    lax.fori_loop(0, owners, build, 0)
    answers[m, me] = outbuf[owners - 1]
    relay(owners, subs, mp_n, me, m, outbuf, answers, (ms, mr), (ss, sr))


def answer(owners, subs, mp_n, cap, mixture, column):
    local = mixture.shape[1]
    dma = pltpu.SemaphoreType.DMA
    side = owners * (mp_n - 1)
    return pl.pallas_call(
        functools.partial(answer_kernel, owners, subs, mp_n),
        out_shape=jax.ShapeDtypeStruct((mp_n, owners, cap, local), bf16),
        in_specs=[VMEM] * 2,
        out_specs=VMEM,
        scratch_shapes=[
            pltpu.VMEM((owners, cap, local), bf16),
            pltpu.VMEM((cap, local), f32),
            dma((owners,)), dma((owners,)), dma((side,)), dma((side,)),
        ],
        compiler_params=pltpu.CompilerParams(collective_id=1, has_side_effects=True),
        name="answer",
    )(mixture, column)


def pick(value, which, pieces):
    part = value.shape[1] // pieces
    out = value[:, :part]
    for j in range(1, pieces):
        out = jnp.where(which == j, value[:, j * part : (j + 1) * part], out)
    return out


def ffn_kernel(
    mp_n, block, voxels, index, answers, w_out, gain, w_up, w_down, result,
    sendbuf, recvbuf, mine, ss, sr,
):
    m = lax.axis_index("mp")
    rows = voxels.shape[0]
    steps = rows // block
    total = answers.shape[1]
    barrier = pltpu.get_barrier_semaphore()
    for p in range(1, mp_n):
        pl.semaphore_signal(
            barrier, inc=1, device_id={"mp": (m + p) % mp_n}, device_id_type=MESH
        )
    pl.semaphore_wait(barrier, mp_n - 1)

    def copy(b, p):
        span = pl.ds(b * block, block)
        return to_mp(
            sendbuf.at[p - 1, span], recvbuf.at[p - 1, span], (ss, sr),
            b * (mp_n - 1) + p - 1, (m + p) % mp_n,
        )

    def work(b, carry):
        span = pl.ds(b * block, block)
        hit = one_hot(index[span, :] == iota((block, total), 1))
        after = voxels[span, :].astype(f32)
        for h in range(mp_n):
            after += dot(dot(hit, answers[h]).astype(bf16), w_out[h])
        normed = normalize(after, gain[...]).astype(bf16)
        hidden = jax.nn.gelu(dot(normed, w_up[...]), approximate=True).astype(bf16)
        terms = dot(hidden, w_down[...])
        mine[span, :] = pick(after, m, mp_n) + pick(terms, m, mp_n)
        for p in range(1, mp_n):
            sendbuf[p - 1, span, :] = pick(terms, (m + p) % mp_n, mp_n).astype(bf16)

        @pl.when(b > 0)
        def _():
            for p in range(1, mp_n):
                copy(b - 1, p).start()

        return carry

    lax.fori_loop(0, steps, work, 0)
    for p in range(1, mp_n):
        copy(steps - 1, p).start()

    def finish(b, carry):
        span = pl.ds(b * block, block)
        out = mine[span, :]
        for p in range(1, mp_n):
            copy(b, p).wait()
            out += recvbuf[p - 1, span, :].astype(f32)
        result[span, :] = out.astype(bf16)
        return carry

    lax.fori_loop(0, steps, finish, 0)


def ffn(mp_n, voxels, index, answers, w_out, gain, w_up, w_down):
    rows, width = voxels.shape
    part = width // mp_n
    block = math.gcd(rows, 256)
    dma = pltpu.SemaphoreType.DMA
    side = rows // block * (mp_n - 1)
    return pl.pallas_call(
        functools.partial(ffn_kernel, mp_n, block),
        out_shape=jax.ShapeDtypeStruct((rows, part), bf16),
        in_specs=[VMEM] * 7,
        out_specs=VMEM,
        scratch_shapes=[
            pltpu.VMEM((mp_n - 1, rows, part), bf16),
            pltpu.VMEM((mp_n - 1, rows, part), bf16),
            pltpu.VMEM((rows, part), f32),
            dma((side,)), dma((side,)),
        ],
        compiler_params=pltpu.CompilerParams(collective_id=2, has_side_effects=True),
        name="ffn",
    )(voxels, index, answers, w_out, gain, w_up, w_down)


def shards(
    subs,
    voxels,
    window_ids,
    voxel_slots,
    window_counts,
    norm_gain,
    w_query_key,
    w_value,
    w_out,
    ffn_gain,
    w_up,
    w_down,
):
    owners = lax.axis_size(("space", "sub"))
    my_index = lax.axis_index(("space", "sub"))
    mp_n = lax.axis_size("mp")
    rows, width = voxels.shape
    cap = 2 * rows // owners
    part = width // mp_n
    normed = normalize(voxels.astype(f32), norm_gain).astype(bf16)
    half = lax.dynamic_slice_in_dim(normed, lax.axis_index("mp") * part, part, 1)
    destination = window_ids // WIN_DEV
    position = window_ids % WIN_DEV * WLEN + voxel_slots
    target = (jnp.arange(owners, dtype=jnp.int32)[:, None] == destination[None, :]).astype(
        jnp.int32
    )
    before = jnp.sum((jnp.cumsum(target, axis=1) - target) * target, axis=0)
    send_index = destination * cap + before
    digits = jnp.stack(
        [position // BASE, position % BASE, jnp.ones_like(position)]
        + [jnp.zeros_like(position)] * 5
    ).astype(bf16)
    arrived, spots, whole_out = dispatch(
        owners, subs, mp_n, cap, half, send_index[None, :], digits, w_out
    )
    counts = lax.dynamic_slice_in_dim(window_counts, my_index * WIN_DEV, WIN_DEV, 0)
    mixture = attend(
        counts, spots.reshape(1, owners * cap), arrived.reshape(mp_n, owners * cap, part),
        w_query_key, w_value,
    )
    answers = answer(owners, subs, mp_n, cap, mixture, spots.reshape(owners, cap, 1))
    return ffn(
        mp_n, voxels, send_index[:, None],
        answers.reshape(mp_n, owners * cap, answers.shape[-1]),
        whole_out, ffn_gain[None, :], w_up, w_down,
    )


def solution(mesh):
    return jax.shard_map(
        functools.partial(shards, mesh.shape["sub"]),
        mesh=mesh,
        in_specs=(
            P(("groups", "space", "sub"), None),
            P(("groups", "space", "sub")),
            P(("groups", "space", "sub")),
            P("groups"),
            P(),
            P(None, None, "mp"),
            P(None, "mp"),
            P("mp", None),
            P(),
            P(None, "mp"),
            P("mp", None),
        ),
        out_specs=P(("groups", "space", "sub"), "mp"),
        check_vma=False,
    )
```

time: 342 us -> 197 us (0.58)
  Pallas kernels: 0 us -> 183 us
  waiting for transfers between devices: 149 us -> 0 us
  local copies, waits for them, and re-layouts: 83.5 us -> 7.79 us
  matrix products: 40.4 us -> 0 us
  other arithmetic: 26.9 us -> 6.21 us
  starting transfers between devices: 16.4 us -> 0 us
  between operations: 13.6 us -> 0.17 us
  blocking collectives: 8.94 us -> 0 us
    pallas_call x0 -> x4, Pallas kernels: none -> 183 us  [the longest x1 62.3 us: answer(): pl.pallas_call(functools.partial(answer_kernel, owners, subs, mp_n), out_...]
    all_to_all x3 -> x0, waiting for transfers between devices: 104 us -> none  [the longest x1 68.9 us: regroup(): lax.all_to_all(send_rows, ('space', 'sub'), split_axis=0, concat_axis=0,...]
    dot_general x7 -> x0, matrix products: 40.4 us -> none  [the longest x1 11.5 us: attend(): jnp.einsum('wqhd,wkhd->whqk', queries.reshape(split_shape), key_rows.resh...]
    scatter x3 -> x0, local copies, waits for them, and re-layouts: 33.5 us -> none  [the longest x1 16.9 us: shards(): padded = jnp.zeros((WIN_DEV * WLEN, row_width), jnp.bfloat16).at[arrived_...]
    reduce_scatter x1 -> x0, waiting for transfers between devices: 26.3 us -> none  [shards(): lax.psum_scatter(ffn_terms.astype(jnp.bfloat16), 'mp', scatter_dimension=...]
    reshape x5 -> x1, local copies, waits for them, and re-layouts: 24.2 us -> 1.52 us  [shards(): spots.reshape(owners, cap, 1)]
    sub x1 -> x0, other arithmetic: 18.8 us -> none  [attend(): weights = jnp.exp(scores - row_max)]
    gather x2 -> x0, local copies, waits for them, and re-layouts: 18.3 us -> none  [the longest x1 13 us: shards(): jnp.take(mixture, arrived_spots, axis=0, mode='clip')]
  transfers between devices with their start and end apart: 5 -> 0, of which waited for: 4 -> 0; matrix products, arithmetic and copies ran while one was open for 5% -> 0% of each run, Pallas kernels for 0% -> 0%
where the time goes in v1:
time: 197 us
  Pallas kernels  183 us (93%)
  local copies, waits for them, and re-layouts  7.79 us (4%)
  other arithmetic  6.21 us (3%)
    pallas_call x1, Pallas kernels, answer(): pl.pallas_call(functools.partial(answer_kernel, owners, subs, mp_n), out_...  62.3 us
    pallas_call x1, Pallas kernels, dispatch(): pl.pallas_call(functools.partial(dispatch_kernel, owners, subs, mp_n), ou...  58.2 us
    pallas_call x1, Pallas kernels, ffn(): pl.pallas_call(functools.partial(ffn_kernel, mp_n, block), out_shape=jax....  31.3 us
    pallas_call x1, Pallas kernels, attend(): pl.pallas_call(functools.partial(attend_kernel, group), grid=(WIN_DEV //...  30.9 us

profile of v1, /device:TPU:30, one launch (start us, length us, event | category | flops | bytes accessed | tf_op | source)
XLA Modules:
  0.0 196.8 jit_solution(8191190527023151924)
XLA Ops:
  0.0 0.0 copy-start
  0.0 0.9 dynamic-slice
  0.9 1.7 convert_reduce_fusion
  2.6 0.0 copy-done
  2.6 0.7 multiply_reduce_fusion
  3.3 0.0 copy-start.2
  3.3 0.0 copy-start.3
  3.3 0.0 copy-start.4
  3.4 1.2 fusion.1.half
  4.5 0.0 copy-done.2
  4.5 0.0 copy-done.3
  4.6 2.3 %reduce-window.6 = s32[8,12,128]{2,1,0:T(8,128)S(1)} reduce-window(s32[8,12,128]{2,1,0:T(8,128)S(1)} %fusion.2, s32[]{:T(128)} %constant.69.clone.1), window={size=1x1x128 pad=0_0x0_0x127_0}, to_apply=%region_0.0 | reduce-window | flops 1560576 | bytes 98308 | tf_op jit(solution)/shard_map/reduce-window
  6.9 0.3 slice_reduce_fusion
  7.1 0.2 reduce-window.9
  7.3 0.1 select_reduce_fusion
  7.4 0.6 broadcast_in_dim.7.index
  8.1 0.7 stack.18.digits
  8.8 58.2 %dispatch.1 = (bf16[2,8,384,256]{3,2,1,0:T(8,128)(2,1)}, s32[8,1,384]{2,1,0:T(1,128)}, bf16[2,256,512]{2,1,0:T(8,128)(2,1)}) custom-call(bf16[1536,256]{1,0:T(8,128)(2,1)} %fusion.1.half, s32[1,1536]{1,0:T(1,128)} %broadcast_in_dim.7.index, bf16[8,1536]{1,0:T(8,128)(2,1)} %stack.18.digits, bf16[256,512]{1,0:T(8,128)(2,1)} %out_rows.1), custom_call_target="tpu_custom_call" | custom-call | tf_op jit(solution)/shard_map/dispatch/pallas_call | solution.py:167
  67.0 0.0 copy-done.4
  67.0 0.6 dynamic_slice.6.counts
  67.6 0.0 copy-start.1
  67.6 30.9 %attend.1.mixture = bf16[4096,256]{1,0:T(8,128)(2,1)} custom-call(s32[16]{0:T(128)} %dynamic_slice.6.counts, s32[1,3072]{1,0:T(1,128)} %bitcast.11, bf16[2,3072,256]{2,1,0:T(8,128)(2,1)} %bitcast.10, bf16[2,512,256]{2,1,0:T(8,128)(2,1)} %w_qk.1, bf16[512,256]{1,0:T(8,128)(2,1)} %w_v.1), custom_call_target="tpu_custom_call" | custom-call | tf_op jit(solution)/shard_map/attend/pallas_call | solution.py:221
  98.5 0.0 copy-done.1
  98.5 1.5 reshape.55.column
  100.0 62.3 %answer.1 = bf16[2,8,384,256]{3,2,1,0:T(8,128)(2,1)} custom-call(bf16[4096,256]{1,0:T(8,128)(2,1)} %attend.1.mixture, s32[8,384,1]{2,1,0:T(8,128)} %reshape.55.column), custom_call_target="tpu_custom_call" | custom-call | tf_op jit(solution)/shard_map/answer/pallas_call | solution.py:271
  162.3 1.1 broadcast_in_dim.17.index
  163.5 31.3 %ffn.1 = bf16[1536,256]{1,0:T(8,128)(2,1)} custom-call(bf16[1536,512]{1,0:T(8,128)(2,1)} %voxels.1, s32[1536,1]{1,0:T(8,128)} %broadcast_in_dim.17.index, bf16[2,3072,256]{2,1,0:T(8,128)(2,1)} %bitcast.9, bf16[2,256,512]{2,1,0:T(8,128)(2,1)} %get-tuple-element.10.w_out, f32[1,512]{1,0:T(1,128)} %bitcast.13, bf16[512,1024]{1,0:T(8,128)(2,1)} %w_up.1, ...), custom_call_target="tpu_custom_call" | custom-call | tf_op jit(solution)/shard_map/ffn/pallas_call | solution.py:358
  194.8 2.1 %copy.15 = bf16[1536,256]{1,0:T(8,128)(2,1)} copy(bf16[1536,256]{1,0:T(8,128)(2,1)} %ffn.1) | data formatting | bytes 1572864
  (12 shorter events, 0.1 us)
Async XLA Ops:
  0.0 2.6 %copy-start = (bf16[1536,512]{1,0:T(8,128)(2,1)S(1)}, bf16[1536,512]{1,0:T(8,128)(2,1)}, u32[]{:S(2)}) copy-start(bf16[1536,512]{1,0:T(8,128)(2,1)} %voxels.1) | copy-start | bytes 4718596
  3.3 1.2 copy-start.2
  3.3 1.2 copy-start.3
  3.3 63.6 %copy-start.4 = (s32[128]{0:T(128)S(1)}, s32[128]{0:T(128)}, u32[]{:S(2)}) copy-start(s32[128]{0:T(128)} %param.14) | copy-start | bytes 1540
  67.6 30.9 %copy-start.1 = (s32[8,1,384]{2,1,0:T(1,128)S(1)}, s32[8,1,384]{2,1,0:T(1,128)}, u32[]{:S(2)}) copy-start(s32[8,1,384]{2,1,0:T(1,128)} %get-tuple-element.8) | copy-start | bytes 36868

commit v2 on v1

v2 whole, which is shorter than its diff:
```python
import functools
import math

import jax
import jax.numpy as jnp
from jax import lax
from jax.experimental import pallas as pl
from jax.experimental.pallas import tpu as pltpu
from jax.sharding import PartitionSpec as P

HDIM = 64
WLEN = 256
WIN_DEV = 16
BASE = 64
MESH = pl.DeviceIdType.MESH
VMEM = pl.BlockSpec(memory_space=pltpu.VMEM)
f32 = jnp.float32
bf16 = jnp.bfloat16


def normalize(values_in, gain):
    row_mean = jnp.mean(values_in, axis=-1, keepdims=True)
    centred = values_in - row_mean
    variance = jnp.mean(centred * centred, axis=-1, keepdims=True)
    return centred * lax.rsqrt(variance + 1e-05) * gain


def iota(shape, dim):
    return lax.broadcasted_iota(jnp.int32, shape, dim)


def one_hot(found):
    return jnp.where(found, f32(1), f32(0)).astype(bf16)


def dot(a, b, dims=((1,), (0,))):
    return lax.dot_general(a, b, (dims, ((), ())), preferred_element_type=f32)


def greet(owners, subs, mp_n, me, m):
    barrier = pltpu.get_barrier_semaphore()
    for k in range(1, owners):
        t = (me + k) % owners
        pl.semaphore_signal(
            barrier, inc=1, device_id={"space": t // subs, "sub": t % subs}, device_id_type=MESH
        )
    for p in range(1, mp_n):
        pl.semaphore_signal(
            barrier, inc=1, device_id={"mp": (m + p) % mp_n}, device_id_type=MESH
        )
    pl.semaphore_wait(barrier, owners - 1 + mp_n - 1)


def to_owner(src, dst, sems, slot, target, subs):
    return pltpu.make_async_remote_copy(
        src_ref=src,
        dst_ref=dst,
        send_sem=sems[0].at[slot],
        recv_sem=sems[1].at[slot],
        device_id={"space": target // subs, "sub": target % subs},
        device_id_type=MESH,
    )


def to_mp(src, dst, sems, index, peer):
    return pltpu.make_async_remote_copy(
        src_ref=src,
        dst_ref=dst,
        send_sem=sems[0].at[index],
        recv_sem=sems[1].at[index],
        device_id={"mp": peer},
        device_id_type=MESH,
    )


def dispatch_kernel(
    spaces, subs, mp_n, normed, index, digits, out_rows, padded, spots, whole_out,
    outbuf, nearbuf, arrived, spotbuf, ms, mr, ps, pr, ss, sr, ws, wr,
):
    owners = spaces * subs
    far = owners - subs
    sp, sb, m = lax.axis_index("space"), lax.axis_index("sub"), lax.axis_index("mp")
    me = sp * subs + sb
    cap, part, rows = outbuf.shape[1], outbuf.shape[2], normed.shape[0]
    greet(owners, subs, mp_n, me, m)
    for p in range(1, mp_n):
        to_mp(out_rows, whole_out.at[m], (ws, wr), p - 1, (m + p) % mp_n).start()
    whole_out[m] = out_rows[...]

    def sink(slot):
        return (sp + slot // subs + 1) % spaces * subs + (sb + slot % subs) % subs

    def source(slot):
        return (sp + spaces - slot // subs - 1) % spaces * subs + (sb + subs - slot % subs) % subs

    def find(slot, t):
        hit = one_hot(index[...] == iota((cap, rows), 0) + t * cap)
        parts = dot(digits[...], hit, ((1,), (1,)))
        place = parts[0:1] * BASE + parts[1:2] + (1 - parts[2:3]) * (WIN_DEV * WLEN)
        spotbuf[slot] = place.astype(jnp.int32)
        return hit

    def spot_copy(slot, s, t):
        return to_owner(spotbuf.at[slot], spots.at[s], (ps, pr), slot, t, subs)

    def far_copy(slot, s, t):
        return to_owner(outbuf.at[slot], arrived.at[s, m], (ms, mr), slot, t, subs)

    def near_copy(j, s, t):
        return to_owner(nearbuf.at[j], arrived.at[s], (ms, mr), far + j, t, subs)

    def side_copy(slot, p, half, s):
        return to_mp(
            arrived.at[s, m], arrived.at[s, half], (ss, sr), slot * (mp_n - 1) + p - 1,
            (m + p) % mp_n,
        )

    def send(slot):
        far_copy(slot, me, sink(slot)).start()
        spot_copy(slot, me, sink(slot)).start()

    def build(slot, carry):
        hit = find(slot, sink(slot))
        mine = normed[:, pl.ds(pl.multiple_of(m * part, part), part)]
        outbuf[slot] = dot(hit, mine).astype(bf16)

        @pl.when(slot > 0)
        def _():
            send(slot - 1)

        return carry

    lax.fori_loop(0, far, build, 0)
    for j in range(subs):
        hit = find(far + j, sp * subs + (sb + j) % subs)
        for h in range(mp_n):
            nearbuf[j, h] = dot(hit, normed[:, h * part : (h + 1) * part]).astype(bf16)
        if j == 0:
            send(far - 1)
        elif j > 1:
            near_copy(j - 1, me, sp * subs + (sb + j - 1) % subs).start()
            spot_copy(far + j - 1, me, sp * subs + (sb + j - 1) % subs).start()
    spots[me] = spotbuf[far]
    chunk = 4 * WLEN

    def put(s, blocks, first):
        row = spots[s]

        def span(c, carry):
            hit = one_hot(row == iota((chunk, cap), 0) + c * chunk)
            here = pl.ds(c * chunk, chunk)
            for h in range(mp_n):
                new = dot(hit, blocks[h]).astype(bf16)
                if not first:
                    new += padded[here, h * part : (h + 1) * part]
                padded[here, h * part : (h + 1) * part] = new
            return carry

        lax.fori_loop(0, padded.shape[0] // chunk, span, 0)

    put(me, nearbuf.at[0], True)
    for j in range(max(subs - 1, 1), subs):
        near_copy(j, me, sp * subs + (sb + j) % subs).start()
        spot_copy(far + j, me, sp * subs + (sb + j) % subs).start()

    def settle(slot):
        s = source(slot)
        for p in range(1, mp_n):
            side_copy(slot, p, (m + mp_n - p) % mp_n, s).wait()
        spot_copy(slot, s, s).wait()
        put(s, arrived.at[s], False)

    def onward(slot, carry):
        s = source(slot)
        far_copy(slot, s, s).wait()
        for p in range(1, mp_n):
            side_copy(slot, p, m, s).start()

        @pl.when(slot > 0)
        def _():
            settle(slot - 1)

        return carry

    lax.fori_loop(0, far, onward, 0)
    for j in range(1, subs):
        s = sp * subs + (sb + subs - j) % subs
        near_copy(j, s, s).wait()
        spot_copy(far + j, s, s).wait()
        put(s, arrived.at[s], False)
    settle(far - 1)
    for p in range(1, mp_n):
        to_mp(
            out_rows, whole_out.at[(m + mp_n - p) % mp_n], (ws, wr), p - 1, (m + p) % mp_n
        ).wait()


def dispatch(spaces, subs, mp_n, cap, normed, index, digits, out_rows):
    owners = spaces * subs
    width = normed.shape[1]
    part = width // mp_n
    dma = pltpu.SemaphoreType.DMA
    side = owners * (mp_n - 1)
    return pl.pallas_call(
        functools.partial(dispatch_kernel, spaces, subs, mp_n),
        out_shape=(
            jax.ShapeDtypeStruct((WIN_DEV * WLEN, width), bf16),
            jax.ShapeDtypeStruct((owners, 1, cap), jnp.int32),
            jax.ShapeDtypeStruct((mp_n,) + out_rows.shape, bf16),
        ),
        in_specs=[VMEM] * 4,
        out_specs=(VMEM, VMEM, VMEM),
        scratch_shapes=[
            pltpu.VMEM((owners - subs, cap, part), bf16),
            pltpu.VMEM((subs, mp_n, cap, part), bf16),
            pltpu.VMEM((owners, mp_n, cap, part), bf16),
            pltpu.VMEM((owners, 1, cap), jnp.int32),
            dma((owners,)), dma((owners,)), dma((owners,)), dma((owners,)),
            dma((side,)), dma((side,)), dma((mp_n,)), dma((mp_n,)),
        ],
        compiler_params=pltpu.CompilerParams(collective_id=0, has_side_effects=True),
        name="dispatch",
    )(normed, index, digits, out_rows)


def attend_kernel(group, counts, padded, w_qk, w_v, mixture):
    step = pl.program_id(0)
    local = w_v.shape[1]
    heads = local // HDIM
    rows_in = padded[...]
    queries = dot(rows_in, w_qk[0]).astype(bf16)
    keys = dot(rows_in, w_qk[1]).astype(bf16)
    values = dot(rows_in, w_v[...]).astype(bf16)
    head_of = iota((1, local), 1) // HDIM
    masks = [jnp.where(head_of == h, f32(1), f32(0)).astype(bf16) for h in range(heads)]
    for g in range(group):
        span = slice(g * WLEN, (g + 1) * WLEN)
        q, k, v = queries[span], keys[span], values[span]
        stacked = jnp.concatenate([q * masks[h] for h in range(heads)], axis=0)
        scores = dot(stacked, k, ((1,), (1,))) * f32(HDIM ** -0.5)
        live = iota((1, WLEN), 1) < counts[step * group + g]
        scores = jnp.where(live, scores, f32(-1e30))
        weights = jnp.exp(scores - jnp.max(scores, axis=-1, keepdims=True))
        scale = 1.0 / jnp.sum(weights, axis=-1, keepdims=True)
        mixed = dot((weights * scale).astype(bf16), v)
        out = mixed[:WLEN]
        for h in range(1, heads):
            out = jnp.where(head_of == h, mixed[h * WLEN : (h + 1) * WLEN], out)
        mixture[span, :] = out.astype(bf16)


def attend(counts, padded, w_qk, w_v, group=2):
    local = w_v.shape[1]
    slots = group * WLEN
    whole = lambda a: pl.BlockSpec(a.shape, lambda i: (0,) * a.ndim)
    return pl.pallas_call(
        functools.partial(attend_kernel, group),
        grid=(WIN_DEV // group,),
        out_shape=jax.ShapeDtypeStruct((WIN_DEV * WLEN, local), bf16),
        in_specs=[
            pl.BlockSpec(memory_space=pltpu.SMEM),
            pl.BlockSpec((slots, padded.shape[1]), lambda i: (i, 0)),
            whole(w_qk),
            whole(w_v),
        ],
        out_specs=pl.BlockSpec((slots, local), lambda i: (i, 0)),
        name="attend",
    )(counts, padded, w_qk, w_v)


def answer_kernel(
    owners, subs, mp_n, mixture, column, index, attended, outbuf, answers, total, ms, mr, ss, sr
):
    me = lax.axis_index("space") * subs + lax.axis_index("sub")
    m = lax.axis_index("mp")
    cap, local = outbuf.shape[1], outbuf.shape[2]
    rows = index.shape[0]
    span = 4 * WLEN
    greet(owners, subs, mp_n, me, m)

    def main_copy(slot, s, t):
        return to_owner(outbuf.at[slot], answers.at[m, s], (ms, mr), slot, t, subs)

    def side_copy(slot, p, src, half, s):
        return to_mp(
            src, answers.at[half, s], (ss, sr), slot * (mp_n - 1) + p - 1, (m + p) % mp_n
        )

    def send(slot):
        t = (me + slot) % owners

        @pl.when(slot > 0)
        def _():
            main_copy(slot, me, t).start()

        @pl.when(slot == 0)
        def _():
            for p in range(1, mp_n):
                side_copy(0, p, outbuf.at[0], m, me).start()

    def onward(slot, carry):
        s = (me + owners - slot) % owners
        main_copy(slot, s, s).wait()
        for p in range(1, mp_n):
            side_copy(slot, p, answers.at[m, s], m, s).start()
        return carry

    def build(slot, carry):
        place = column[(me + slot) % owners]
        total[...] = jnp.zeros_like(total)

        def add(c, inner):
            hit = one_hot(place == iota((cap, span), 1) + c * span)
            total[...] += dot(hit, mixture[pl.ds(c * span, span), :])
            return inner

        lax.fori_loop(0, mixture.shape[0] // span, add, 0)
        outbuf[slot] = total[...].astype(bf16)

        @pl.when(slot > 0)
        def _():
            send(slot - 1)

        @pl.when((slot >= 4) & (slot % 2 == 0))
        def _():
            onward(slot // 2 - 1, 0)

        return carry

    lax.fori_loop(0, owners, build, 0)
    send(owners - 1)
    answers[m, me] = outbuf[0]
    attended[...] = jnp.zeros_like(attended)

    def settle(slot):
        s = (me + owners - slot) % owners
        for p in range(1, mp_n):
            side_copy(slot, p, outbuf.at[slot], (m + mp_n - p) % mp_n, s).wait()
        hit = one_hot(index[...] == iota((rows, cap), 1) + s * cap)
        for h in range(mp_n):
            attended[h] += dot(hit, answers[h, s]).astype(bf16)

    ahead = max((owners - 1) // 2 - 1, 0)

    def drain(slot, carry):
        onward(slot, 0)
        settle(slot - ahead - 1)
        return carry

    lax.fori_loop(ahead + 1, owners, drain, 0)

    def rest(slot, carry):
        settle(slot)
        return carry

    lax.fori_loop(owners - ahead - 1, owners, rest, 0)


def answer(owners, subs, mp_n, cap, mixture, column, index):
    local = mixture.shape[1]
    dma = pltpu.SemaphoreType.DMA
    side = owners * (mp_n - 1)
    return pl.pallas_call(
        functools.partial(answer_kernel, owners, subs, mp_n),
        out_shape=jax.ShapeDtypeStruct((mp_n, index.shape[0], local), bf16),
        in_specs=[VMEM] * 3,
        out_specs=VMEM,
        scratch_shapes=[
            pltpu.VMEM((owners, cap, local), bf16),
            pltpu.VMEM((mp_n, owners, cap, local), bf16),
            pltpu.VMEM((cap, local), f32),
            dma((owners,)), dma((owners,)), dma((side,)), dma((side,)),
        ],
        compiler_params=pltpu.CompilerParams(collective_id=1, has_side_effects=True),
        name="answer",
    )(mixture, column, index)


def pick(value, which, pieces):
    part = value.shape[1] // pieces
    out = value[:, :part]
    for j in range(1, pieces):
        out = jnp.where(which == j, value[:, j * part : (j + 1) * part], out)
    return out


def ffn_kernel(
    mp_n, block, voxels, attended, w_out, gain, w_up, w_down, result,
    sendbuf, recvbuf, mine, ss, sr,
):
    m = lax.axis_index("mp")
    rows = voxels.shape[0]
    steps = rows // block
    barrier = pltpu.get_barrier_semaphore()
    for p in range(1, mp_n):
        pl.semaphore_signal(
            barrier, inc=1, device_id={"mp": (m + p) % mp_n}, device_id_type=MESH
        )
    pl.semaphore_wait(barrier, mp_n - 1)

    def copy(b, p):
        span = pl.ds(b * block, block)
        return to_mp(
            sendbuf.at[p - 1, span], recvbuf.at[p - 1, span], (ss, sr),
            b * (mp_n - 1) + p - 1, (m + p) % mp_n,
        )

    def work(b, carry):
        span = pl.ds(b * block, block)
        after = voxels[span, :].astype(f32)
        for h in range(mp_n):
            after += dot(attended[h, span, :], w_out[h])
        normed = normalize(after, gain[...]).astype(bf16)
        hidden = jax.nn.gelu(dot(normed, w_up[...]), approximate=True).astype(bf16)
        terms = dot(hidden, w_down[...])
        mine[span, :] = pick(after, m, mp_n) + pick(terms, m, mp_n)
        for p in range(1, mp_n):
            sendbuf[p - 1, span, :] = pick(terms, (m + p) % mp_n, mp_n).astype(bf16)

        @pl.when(b > 0)
        def _():
            for p in range(1, mp_n):
                copy(b - 1, p).start()

        return carry

    lax.fori_loop(0, steps, work, 0)
    for p in range(1, mp_n):
        copy(steps - 1, p).start()

    def finish(b, carry):
        span = pl.ds(b * block, block)
        out = mine[span, :]
        for p in range(1, mp_n):
            copy(b, p).wait()
            out += recvbuf[p - 1, span, :].astype(f32)
        result[span, :] = out.astype(bf16)
        return carry

    lax.fori_loop(0, steps, finish, 0)


def ffn(mp_n, voxels, attended, w_out, gain, w_up, w_down):
    rows, width = voxels.shape
    part = width // mp_n
    block = math.gcd(rows, 256)
    dma = pltpu.SemaphoreType.DMA
    side = rows // block * (mp_n - 1)
    return pl.pallas_call(
        functools.partial(ffn_kernel, mp_n, block),
        out_shape=jax.ShapeDtypeStruct((rows, part), bf16),
        in_specs=[VMEM] * 6,
        out_specs=VMEM,
        scratch_shapes=[
            pltpu.VMEM((mp_n - 1, rows, part), bf16),
            pltpu.VMEM((mp_n - 1, rows, part), bf16),
            pltpu.VMEM((rows, part), f32),
            dma((side,)), dma((side,)),
        ],
        compiler_params=pltpu.CompilerParams(collective_id=2, has_side_effects=True),
        name="ffn",
    )(voxels, attended, w_out, gain, w_up, w_down)


def shards(
    subs,
    voxels,
    window_ids,
    voxel_slots,
    window_counts,
    norm_gain,
    w_query_key,
    w_value,
    w_out,
    ffn_gain,
    w_up,
    w_down,
):
    owners = lax.axis_size(("space", "sub"))
    my_index = lax.axis_index(("space", "sub"))
    mp_n = lax.axis_size("mp")
    rows = voxels.shape[0]
    cap = 2 * rows // owners
    normed = normalize(voxels.astype(f32), norm_gain).astype(bf16)
    destination = window_ids // WIN_DEV
    position = window_ids % WIN_DEV * WLEN + voxel_slots
    target = (jnp.arange(owners, dtype=jnp.int32)[:, None] == destination[None, :]).astype(
        jnp.int32
    )
    before = jnp.sum((jnp.cumsum(target, axis=1) - target) * target, axis=0)
    send_index = destination * cap + before
    digits = jnp.stack(
        [position // BASE, position % BASE, jnp.ones_like(position)]
        + [jnp.zeros_like(position)] * 5
    ).astype(bf16)
    padded, spots, whole_out = dispatch(
        owners // subs, subs, mp_n, cap, normed, send_index[None, :], digits, w_out
    )
    counts = lax.dynamic_slice_in_dim(window_counts, my_index * WIN_DEV, WIN_DEV, 0)
    mixture = attend(counts, padded, w_query_key, w_value)
    attended = answer(
        owners, subs, mp_n, cap, mixture, spots.reshape(owners, cap, 1), send_index[:, None]
    )
    return ffn(mp_n, voxels, attended, whole_out, ffn_gain[None, :], w_up, w_down)


def solution(mesh):
    return jax.shard_map(
        functools.partial(shards, mesh.shape["sub"]),
        mesh=mesh,
        in_specs=(
            P(("groups", "space", "sub"), None),
            P(("groups", "space", "sub")),
            P(("groups", "space", "sub")),
            P("groups"),
            P(),
            P(None, None, "mp"),
            P(None, "mp"),
            P("mp", None),
            P(),
            P(None, "mp"),
            P("mp", None),
        ),
        out_specs=P(("groups", "space", "sub"), "mp"),
        check_vma=False,
    )
```

time: 197 us -> 184 us (0.934)
  Pallas kernels: 183 us -> 168 us
  other arithmetic: 6.21 us -> 8.4 us
    pallas_call x1, Pallas kernels: 30.9 us -> 17 us  [attend(): pl.pallas_call(functools.partial(attend_kernel, group), grid=(WIN_DEV //...]
    pallas_call x1, Pallas kernels: 31.3 us -> 25 us  [ffn(): pl.pallas_call(functools.partial(ffn_kernel, mp_n, block), out_shape=jax....]
    pallas_call x1, Pallas kernels: 58.2 us -> 61.6 us  [dispatch(): pl.pallas_call(functools.partial(dispatch_kernel, spaces, subs, mp_n), ou...]
    pallas_call x1, Pallas kernels: 62.3 us -> 64.8 us  [answer(): pl.pallas_call(functools.partial(answer_kernel, owners, subs, mp_n), out_...]
where the time goes in v2:
time: 184 us
  Pallas kernels  168 us (91%)
  other arithmetic  8.4 us (5%)
  local copies, waits for them, and re-layouts  6.86 us (4%)
    pallas_call x1, Pallas kernels, answer(): pl.pallas_call(functools.partial(answer_kernel, owners, subs, mp_n), out_...  64.8 us
    pallas_call x1, Pallas kernels, dispatch(): pl.pallas_call(functools.partial(dispatch_kernel, spaces, subs, mp_n), ou...  61.6 us
    pallas_call x1, Pallas kernels, ffn(): pl.pallas_call(functools.partial(ffn_kernel, mp_n, block), out_shape=jax....  25 us
    pallas_call x1, Pallas kernels, attend(): pl.pallas_call(functools.partial(attend_kernel, group), grid=(WIN_DEV //...  17 us

profile of v2, /device:TPU:30, one launch (start us, length us, event | category | flops | bytes accessed | tf_op | source)
XLA Modules:
  0.0 183.9 jit_solution(1475353360346023475)
XLA Ops:
  0.0 0.0 copy-start
  0.0 0.0 copy-start.2
  0.0 0.9 fusion.9
  0.9 2.3 %reduce-window.6 = s32[8,12,128]{2,1,0:T(8,128)S(1)} reduce-window(s32[8,12,128]{2,1,0:T(8,128)S(1)} %fusion.5, s32[]{:T(128)} %constant.69.clone.1), window={size=1x1x128 pad=0_0x0_0x127_0}, to_apply=%region_2.3 | reduce-window | flops 1560576 | bytes 98308 | tf_op jit(solution)/shard_map/reduce-window
  3.2 0.3 slice_reduce_fusion
  3.4 0.2 reduce-window.9
  3.6 0.1 select_reduce_fusion
  3.7 0.7 bitcast_add_fusion
  4.4 0.6 broadcast_in_dim.6.index
  5.1 0.7 stack.18.digits
  5.8 1.7 convert_reduce_fusion
  7.5 0.0 copy-done
  7.5 0.0 copy-start.3
  7.5 0.8 fusion.2
  8.3 0.0 copy-done.2
  8.3 1.8 fusion.4.normed
  10.1 61.6 %dispatch.1 = (bf16[4096,512]{1,0:T(8,128)(2,1)}, s32[8,1,384]{2,1,0:T(1,128)}, bf16[2,256,512]{2,1,0:T(8,128)(2,1)}) custom-call(bf16[1536,512]{1,0:T(8,128)(2,1)} %fusion.4.normed, s32[1,1536]{1,0:T(1,128)} %broadcast_in_dim.6.index, bf16[8,1536]{1,0:T(8,128)(2,1)} %stack.18.digits, bf16[256,512]{1,0:T(8,128)(2,1)} %out_rows.1), custom_call_target="tpu_custom_call" | custom-call | tf_op jit(solution)/shard_map/dispatch/pallas_call | solution.py:204
  71.7 0.0 copy-done.3
  71.7 0.6 dynamic_slice.3.counts
  72.3 0.0 copy-start.1
  72.3 17.0 %attend.1.mixture = bf16[4096,256]{1,0:T(8,128)(2,1)} custom-call(s32[16]{0:T(128)} %dynamic_slice.3.counts, bf16[4096,512]{1,0:T(8,128)(2,1)} %get-tuple-element.8.padded, bf16[2,512,256]{2,1,0:T(8,128)(2,1)} %w_qk.1, bf16[512,256]{1,0:T(8,128)(2,1)} %w_v.1), custom_call_target="tpu_custom_call" | custom-call | tf_op jit(solution)/shard_map/attend/pallas_call | solution.py:256
  89.3 0.0 copy-done.1
  89.4 1.5 reshape.43.column
  90.8 1.1 broadcast_in_dim.17.index
  92.0 64.8 %answer.1.attended = bf16[2,1536,256]{2,1,0:T(8,128)(2,1)} custom-call(bf16[4096,256]{1,0:T(8,128)(2,1)} %attend.1.mixture, s32[8,384,1]{2,1,0:T(8,128)} %reshape.43.column, s32[1536,1]{1,0:T(8,128)} %broadcast_in_dim.17.index), custom_call_target="tpu_custom_call" | custom-call | tf_op jit(solution)/shard_map/answer/pallas_call | solution.py:363
  156.8 25.0 %ffn.1 = bf16[1536,256]{1,0:T(8,128)(2,1)} custom-call(bf16[1536,512]{1,0:T(8,128)(2,1)} %voxels.1, bf16[2,1536,256]{2,1,0:T(8,128)(2,1)} %answer.1.attended, bf16[2,256,512]{2,1,0:T(8,128)(2,1)} %get-tuple-element.10.w_out, f32[1,512]{1,0:T(1,128)} %bitcast.7, bf16[512,1024]{1,0:T(8,128)(2,1)} %w_up.1, bf16[1024,512]{1,0:T(8,128)(2,1)} %w_down.1), custom_call_target="tpu_custom_call" | custom-call | tf_op jit(solution)/shard_map/ffn/pallas_call | solution.py:449
  181.8 2.1 %copy.15 = bf16[1536,256]{1,0:T(8,128)(2,1)} copy(bf16[1536,256]{1,0:T(8,128)(2,1)} %ffn.1) | data formatting | bytes 1572864
  (10 shorter events, 0.1 us)
Async XLA Ops:
  0.0 7.5 %copy-start = (bf16[1536,512]{1,0:T(8,128)(2,1)S(1)}, bf16[1536,512]{1,0:T(8,128)(2,1)}, u32[]{:S(2)}) copy-start(bf16[1536,512]{1,0:T(8,128)(2,1)} %voxels.1) | copy-start | bytes 4718596
  0.0 8.3 %copy-start.2 = (f32[512]{0:T(512)S(1)}, f32[512]{0:T(512)}, u32[]{:S(2)}) copy-start(f32[512]{0:T(512)} %param.15) | copy-start | bytes 6148
  7.5 64.2 %copy-start.3 = (s32[128]{0:T(128)S(1)}, s32[128]{0:T(128)}, u32[]{:S(2)}) copy-start(s32[128]{0:T(128)} %param.14) | copy-start | bytes 1540
  72.3 17.0 %copy-start.1 = (s32[8,1,384]{2,1,0:T(1,128)S(1)}, s32[8,1,384]{2,1,0:T(1,128)}, u32[]{:S(2)}) copy-start(s32[8,1,384]{2,1,0:T(1,128)} %get-tuple-element.9) | copy-start | bytes 36868
